TPU v7x, 32 devices: a whole 2x2x4 slice. The times are simulated.
32 devices in a mesh: grp: 4 (over x, core), fsdp: 8 (over z, y).
Axes of the slice: x: 2, y: 2, z: 4, core: 2. Of those that a mesh axis runs over, the one named last changes fastest.
Arguments:
- layer_input_rows: bfloat16 [16384, 8192], P(('grp', 'fsdp')), may hold values from -400 to 400, as said below
- input_norm_gain: bfloat16 [8192], replicated, may hold values from 0.5 to 1.5
- key_value_codes: int32 [8192, 256], P('fsdp'), may hold values from 0 to 65535
- block_scale_codes: int32 [256, 128], P('fsdp'), may hold values from -2147483648 to 2147483646
- outer_scale_codes: int32 [512], P('fsdp'), may hold values from 0 to 255
- adapter_down_factor: bfloat16 [8192, 64], replicated, may hold values from -0.0625 to 0.0625
- adapter_up_factor: bfloat16 [64, 1024], replicated, may hold values from -0.75 to 0.75
- target: bfloat16 [16384, 1024], P(('grp', 'fsdp')), may hold values from -18 to 18
Outputs:
- kv: bfloat16 [16384, 1024], P(('grp', 'fsdp'))
- loss: float32 [], replicated
Inputs may be any that keep to these rules, and one draw needn't show every extreme that they name: layer_input_rows rows and features carry varied scales.
All inputs are finite; a program needn't handle non-finite values.
Results may differ from a plain program's by a relative error of at most 0.0057.
Values may be sent and summed in bfloat16 or wider, within the bound.
A program may use at most 128 MiB of HBM per device.

v0:
```python
import functools

import jax
import jax.numpy as jnp
from jax import lax
from jax.experimental import pallas as pl
from jax.experimental.pallas import tpu as pltpu
from jax.sharding import PartitionSpec as P

adapter_scale = 0.25
epsilon = 1e-06
nf4_levels = (
    -1.0,
    -0.6961928009986877,
    -0.5250730514526367,
    -0.39491748809814453,
    -0.28444138169288635,
    -0.18477343022823334,
    -0.09105003625154495,
    0.0,
    0.07958029955625534,
    0.16093020141124725,
    0.24611230194568634,
    0.33791524171066284,
    0.44070982933044434,
    0.5626170039176941,
    0.7229568362236023,
    1.0,
)
MESH = pl.DeviceIdType.MESH


def nibble_levels(words, plane):
    values = [jnp.float32(level) for level in nf4_levels]
    for bit in range(4):
        is_set = jnp.bitwise_and(words, 1 << (4 * plane + bit)) != 0
        values = [
            jnp.where(is_set, values[2 * i + 1], values[2 * i])
            for i in range(len(values) // 2)
        ]
    return values[0]


def kernel(
    layers,
    x_hbm,
    gain_ref,
    codes_ref,
    scales_ref,
    outer_ref,
    down_hbm,
    up_ref,
    target_hbm,
    out_ref,
    loss_ref,
    x_ref,
    weight_ref,
    acc_ref,
    target_ref,
    down_ref,
    spread_ref,
    scale_ref,
    wide_gain_ref,
    plane_ref,
    line_ref,
    local_sem,
    z_send,
    x_send,
    y_send,
    own_send,
    core_send,
    link_recv,
    core_recv,
    plane_send,
    plane_recv,
    line_send,
    line_recv,
):
    g = lax.axis_index("grp")
    f = lax.axis_index("fsdp")
    cx, cc = g // 2, g % 2
    cl, cy = f // 2, f % 2
    tokens, width = x_ref.shape
    columns = acc_ref.shape[1]
    rows = codes_ref.shape[0]
    half = rows // 2
    piece = half // 4

    sibling = (cx * 2 + 1 - cc, f)
    x_peer = ((1 - cx) * 2 + cc, f)
    y_peer = (g, cl * 2 + 1 - cy)

    def z_peer(step):
        return (g, (cl + step) * 2 + cy)

    part = tokens // 4
    x_copies = [
        pltpu.make_async_copy(
            x_hbm.at[pl.ds(p * part, part)], x_ref.at[pl.ds(p * part, part)], local_sem.at[p]
        )
        for p in range(4)
    ]
    target_copy = pltpu.make_async_copy(target_hbm, target_ref, local_sem.at[4])
    down_copy = pltpu.make_async_copy(down_hbm, down_ref, local_sem.at[5])
    for copy in x_copies:
        copy.start()
    down_copy.start()
    target_copy.start()

    barrier = pltpu.get_barrier_semaphore()
    spot = (cx * 2 + cc) * 2 + cy

    def plane_peer(i):
        to = (spot + i) % 8
        return (to // 2, cl * 2 + to % 2)

    def line_peer(i):
        return (g, (cl + i) % layers * 2 + cy)

    for i in range(1, 8):
        pl.semaphore_signal(barrier, inc=1, device_id=plane_peer(i), device_id_type=MESH)

    def greet(i, carry):
        pl.semaphore_signal(barrier, inc=1, device_id=line_peer(i), device_id_type=MESH)
        return carry

    lax.fori_loop(1, layers, greet, 0)

    def mirror(px, j):
        return j + px * (3 - 2 * j)

    def chunk(layer, y, c, q):
        start = ((layer * 2 + y) * 2 + c) * half + q * piece
        return weight_ref.at[pl.ds(pl.multiple_of(start, piece), piece)]

    def slot(layer, y, q):
        return (layer * 2 + y) * 4 + q

    def link_copy(layer, y, q, send_sem, peer):
        ref = chunk(layer, y, cc, q)
        return pltpu.make_async_remote_copy(
            src_ref=ref,
            dst_ref=ref,
            send_sem=send_sem,
            recv_sem=link_recv.at[slot(layer, y, q)],
            device_id=peer,
            device_id_type=MESH,
        )

    def z_copy(layer, j, step):
        sem = z_send.at[(1 + step) // 2 * (layers * 3) + layer * 3 + j]
        return link_copy(layer, cy, mirror(cx, j), sem, z_peer(step))

    def xz_copy(layer):
        return link_copy(layer, cy, mirror(cx, 0), x_send.at[layer * 3], x_peer)

    def xy_copy(layer, j):
        return link_copy(layer, 1 - cy, mirror(cx, j), x_send.at[layer * 3 + 1 + j], x_peer)

    def y_copy(layer, j):
        return link_copy(layer, cy, mirror(cx, j), y_send.at[layer * 2 + j], y_peer)

    def own_copy(k):
        return link_copy(cl, cy, mirror(cx, k), own_send.at[k], y_peer)

    def core_copy(layer, y, q):
        ref = chunk(layer, y, cc, q)
        place = slot(layer, y, q)
        return pltpu.make_async_remote_copy(
            src_ref=ref,
            dst_ref=ref,
            send_sem=core_send.at[place],
            recv_sem=core_recv.at[place],
            device_id=sibling,
            device_id_type=MESH,
        )

    def arrived(layer, y, q):
        ref = chunk(layer, y, cc, q)
        pltpu.make_async_copy(ref, ref, link_recv.at[slot(layer, y, q)]).wait()

    def core_arrived(layer, y, q):
        ref = chunk(layer, y, 1 - cc, q)
        pltpu.make_async_copy(ref, ref, core_recv.at[slot(layer, y, q)]).wait()

    wide_gain_ref[...] = gain_ref[...].astype(jnp.float32)

    words = codes_ref.shape[1]
    lanes = scales_ref.shape[1]
    per_row = scales_ref.shape[0] * lanes // rows
    line = rows // scales_ref.shape[0]
    row = lax.broadcasted_iota(jnp.int32, (rows, lanes), 0)
    lane = lax.broadcasted_iota(jnp.int32, (rows, lanes), 1)
    mine = lane // per_row == row % line
    place = lax.broadcasted_iota(jnp.int32, (lanes, words), 0)
    word = lax.broadcasted_iota(jnp.int32, (lanes, words), 1)
    run = words // (4 * per_row)
    code = jnp.zeros((rows, words), jnp.float32)
    scale_words = jnp.concatenate(
        [
            jnp.broadcast_to(scales_ref[pl.ds(i, 1), :], (line, lanes))
            for i in range(scales_ref.shape[0])
        ],
        axis=0,
    )
    for byte in range(4):
        value = jnp.bitwise_and(jnp.right_shift(scale_words, 8 * byte), 255)
        value = jnp.where(mine, value.astype(jnp.float32), 0.0).astype(jnp.bfloat16)
        pick = (place % per_row == word // (4 * run)) & ((word // run) % 4 == byte)
        code += jnp.dot(
            value,
            jnp.where(pick, 1.0, 0.0).astype(jnp.bfloat16),
            preferred_element_type=jnp.float32,
        )
    outer_count = outer_ref.shape[1]
    outer_rows = rows // outer_count
    outer_row = lax.broadcasted_iota(jnp.int32, (rows, outer_count), 0)
    outer_lane = lax.broadcasted_iota(jnp.int32, (rows, outer_count), 1)
    second = jnp.sum(
        jnp.where(
            outer_row // outer_rows == outer_lane, outer_ref[...].astype(jnp.float32), 0.0
        ),
        axis=1,
        keepdims=True,
    )
    second = jnp.exp2(second / 128.0 - 6.0)
    scale_ref[...] = (code + 0.5) / 256.0 * second

    deep = lax.broadcasted_iota(jnp.int32, spread_ref.shape, 0)
    wide = lax.broadcasted_iota(jnp.int32, spread_ref.shape, 1)
    spread_ref[...] = jnp.where(
        (deep % 128) * 4 + deep // 128 == wide, 1.0, 0.0
    ).astype(jnp.bfloat16)

    def decode(start):
        start = pl.multiple_of(start, piece)
        for h in range(words // 128):
            span = pl.ds(h * 128, 128)
            code_words = codes_ref[pl.ds(start, piece), span]
            scale = scale_ref[pl.ds(start, piece), span]
            planes = [
                (nibble_levels(code_words, plane) * scale).astype(jnp.bfloat16)
                for plane in range(4)
            ]
            ordered = jnp.dot(
                jnp.concatenate(planes, axis=1),
                spread_ref[...],
                preferred_element_type=jnp.float32,
            )
            weight_ref[
                pl.ds(pl.multiple_of(f * rows + start, piece), piece), pl.ds(h * 512, 512)
            ] = ordered.astype(jnp.bfloat16)

    decode(cc * half + mirror(cx, 0) * piece)
    pl.semaphore_wait(barrier, 7 + layers - 1)

    def first_sends(j):
        @pl.when(cl > 0)
        def _():
            z_copy(cl, j, -1).start()

        @pl.when(cl < layers - 1)
        def _():
            z_copy(cl, j, 1).start()

        pl.when(j == 0)(lambda: own_copy(0).start())

    def rest(j, carry):
        decode(cc * half + mirror(cx, j) * piece)
        first_sends(j - 1)
        return carry

    lax.fori_loop(1, 4, rest, 0)
    for k in range(layers, 4):
        own_copy(k).start()

    def other(j, carry):
        decode((1 - cc) * half + j * piece)
        return carry

    lax.fori_loop(0, 4, other, 0)

    block = min(16, part)
    tile = min(1024, width)

    def normalize(p):
        x_copies[p].wait()

        def some(i, carry):
            at = pl.ds(pl.multiple_of(p * part + i * block, block), block)
            total = jnp.zeros((block, 128), jnp.float32)
            for t in range(width // tile):
                v = x_ref[at, pl.ds(t * tile, tile)].astype(jnp.float32)
                v = v * v
                for k in range(tile // 128):
                    total += v[:, k * 128 : (k + 1) * 128]
            inverse = lax.rsqrt(jnp.sum(total, axis=1, keepdims=True) / width + epsilon)
            for t in range(width // 128):
                span = pl.ds(t * 128, 128)
                v = x_ref[at, span].astype(jnp.float32)
                x_ref[at, span] = (v * inverse * wide_gain_ref[pl.ds(t, 1), :]).astype(jnp.bfloat16)
            return carry

        lax.fori_loop(0, part // block, some, 0)

    def adapter():
        down_copy.wait()
        low = lax.dot_general(
            x_ref[...],
            down_ref[...],
            (((1,), (1,)), ((), ())),
            preferred_element_type=jnp.float32,
        )
        acc_ref[...] = adapter_scale * jnp.dot(
            low.astype(jnp.bfloat16), up_ref[...], preferred_element_type=jnp.float32
        )

    across = min(256, columns)

    def multiply(layer, y):
        at = pl.ds(pl.multiple_of((layer * 2 + y) * rows, rows), rows)

        def some(n, carry):
            cols = pl.ds(pl.multiple_of(n * across, across), across)
            acc_ref[:, cols] += jnp.dot(
                x_ref[:, at], weight_ref[at, cols], preferred_element_type=jnp.float32
            )
            return carry

        lax.fori_loop(0, columns // across, some, 0)

    def multiply_arrived(layer, y):
        for q in range(4):
            core_arrived(layer, y, q)
        multiply(layer, y)

    def both(s, act):
        for step in (-1, 1):
            layer = cl + step * s
            pl.when((layer >= 0) & (layer < layers))(functools.partial(act, layer, step))

    def z_event(s, j):
        def act(layer, step):
            arrived(layer, cy, mirror(cx, j))
            onward = cl - step

            @pl.when((onward >= 0) & (onward < layers))
            def _():
                z_copy(layer, j, -step).start()

            if j == 0:
                xz_copy(layer).start()
            if j < 2:
                y_copy(layer, j).start()
            core_copy(layer, cy, mirror(cx, j)).start()

        both(s, act)

    def y_event(s, j):
        def act(layer, step):
            q = mirror(cx, j)
            arrived(layer, 1 - cy, q)
            xy_copy(layer, j).start()
            core_copy(layer, 1 - cy, q).start()

        both(s, act)

    def xz_event(s):
        def act(layer, step):
            q = mirror(1 - cx, 0)
            arrived(layer, cy, q)
            core_copy(layer, cy, q).start()

        both(s, act)

    def xy_event(s, j):
        def act(layer, step):
            q = mirror(1 - cx, j)
            arrived(layer, 1 - cy, q)
            core_copy(layer, 1 - cy, q).start()

        both(s, act)

    def own_event(k):
        q = mirror(cx, k)
        arrived(cl, 1 - cy, q)
        core_copy(cl, 1 - cy, q).start()

    def late(s):
        pl.when(s <= 4)(lambda: own_event(s - 1))
        xy_event(s - 1, 0)
        xy_event(s - 1, 1)

    def one_step(s, carry):
        z_event(s, 0)

        @pl.when(s > 1)
        def _():
            both(s - 1, lambda layer, step: multiply_arrived(layer, cy))

        @pl.when(s == 1)
        def _():
            normalize(0)
            normalize(1)

        z_event(s, 1)
        y_event(s, 0)
        pl.when(s > 1)(lambda: late(s))
        pl.when(s == 1)(lambda: own_event(0))

        @pl.when(s == 1)
        def _():
            normalize(2)
            normalize(3)

        z_event(s, 2)
        pl.when(s < 4)(lambda: own_copy(s).start())
        y_event(s, 1)
        xz_event(s)

        @pl.when(s > 1)
        def _():
            both(s - 1, lambda layer, step: multiply_arrived(layer, 1 - cy))

        @pl.when(s == 1)
        def _():
            adapter()
            multiply(cl, cy)

        return carry

    lax.fori_loop(1, layers, one_step, 0)
    xy_event(layers - 1, 0)
    both(layers - 1, lambda layer, step: multiply_arrived(layer, cy))
    for k in range(min(layers - 1, 4), 4):
        own_event(k)
    xy_event(layers - 1, 1)
    multiply_arrived(cl, 1 - cy)
    both(layers - 1, lambda layer, step: multiply_arrived(layer, 1 - cy))

    target_copy.wait()
    plane_ref[spot] = jnp.zeros((8, 128), jnp.float32)

    def finish(i, carry):
        at = pl.ds(pl.multiple_of(i * block, block), block)
        exact = acc_ref[at, :]
        out_ref[at, :] = exact.astype(jnp.bfloat16)
        error = exact - target_ref[at, :].astype(jnp.float32)
        error = error * error
        total = jnp.zeros((block, 128), jnp.float32)
        for k in range(columns // 128):
            total += error[:, k * 128 : (k + 1) * 128]
        for k in range(block // 8):
            plane_ref[spot] += total[k * 8 : (k + 1) * 8]
        return carry

    lax.fori_loop(0, tokens // block, finish, 0)

    for j in range(3):
        for step in (-1, 1):

            @pl.when((cl + step >= 0) & (cl + step < layers))
            def _():
                z_copy(cl, j, step).wait_send()

    def sent(s, carry):
        def act(layer, step):
            onward = cl - step

            @pl.when((onward >= 0) & (onward < layers))
            def _():
                for j in range(3):
                    z_copy(layer, j, -step).wait_send()

            xz_copy(layer).wait_send()
            for j in range(2):
                y_copy(layer, j).wait_send()
                xy_copy(layer, j).wait_send()
            for q in range(4):
                core_copy(layer, cy, q).wait_send()
                core_copy(layer, 1 - cy, q).wait_send()

        both(s, act)
        return carry

    lax.fori_loop(1, layers, sent, 0)
    for k in range(4):
        own_copy(k).wait_send()
        core_copy(cl, 1 - cy, k).wait_send()

    def plane_copy(i):
        return pltpu.make_async_remote_copy(
            src_ref=plane_ref.at[spot],
            dst_ref=plane_ref.at[spot],
            send_sem=plane_send.at[i],
            recv_sem=plane_recv.at[spot],
            device_id=plane_peer(i),
            device_id_type=MESH,
        )

    def line_copy(i):
        return pltpu.make_async_remote_copy(
            src_ref=line_ref.at[cl],
            dst_ref=line_ref.at[cl],
            send_sem=line_send.at[i],
            recv_sem=line_recv.at[cl],
            device_id=line_peer(i),
            device_id_type=MESH,
        )

    def landed(ref, sem):
        pltpu.make_async_copy(ref, ref, sem).wait()

    for i in range(1, 8):
        plane_copy(i).start()
    for i in range(1, 8):
        source = (spot + i) % 8
        landed(plane_ref.at[source], plane_recv.at[source])
    line_ref[cl] = jnp.sum(plane_ref[...], axis=0)
    for i in range(1, 8):
        plane_copy(i).wait_send()

    def to_line(i, carry):
        line_copy(i).start()
        return carry

    def from_line(i, carry):
        source = (cl + i) % layers
        landed(line_ref.at[source], line_recv.at[source])
        line_copy(i).wait_send()
        return carry

    lax.fori_loop(1, layers, to_line, 0)
    lax.fori_loop(1, layers, from_line, 0)
    loss_ref[0, 0] = jnp.sum(line_ref[...]) / (tokens * layers * 2 * columns)


def per_device(fsdp, x, gain, codes, scales, outer, down, up, target):
    tokens, width = x.shape
    columns = up.shape[1]
    rows = codes.shape[0]
    layers = fsdp // 2
    vmem = pl.BlockSpec(memory_space=pltpu.VMEM)
    anywhere = pl.BlockSpec(memory_space=pl.ANY)
    dma = pltpu.SemaphoreType.DMA
    kv, loss = pl.pallas_call(
        functools.partial(kernel, layers),
        out_shape=(
            jax.ShapeDtypeStruct((tokens, columns), jnp.bfloat16),
            jax.ShapeDtypeStruct((1, 1), jnp.float32),
        ),
        in_specs=[anywhere, vmem, vmem, vmem, vmem, anywhere, vmem, anywhere],
        out_specs=(vmem, pl.BlockSpec(memory_space=pltpu.SMEM)),
        scratch_shapes=[
            pltpu.VMEM((tokens, width), jnp.bfloat16),
            pltpu.VMEM((width, columns), jnp.bfloat16),
            pltpu.VMEM((tokens, columns), jnp.float32),
            pltpu.VMEM((tokens, columns), jnp.bfloat16),
            pltpu.VMEM(down.shape[::-1], jnp.bfloat16),
            pltpu.VMEM((512, 512), jnp.bfloat16),
            pltpu.VMEM(codes.shape, jnp.float32),
            pltpu.VMEM((width // 128, 128), jnp.float32),
            pltpu.VMEM((8, 8, 128), jnp.float32),
            pltpu.VMEM((layers, 8, 128), jnp.float32),
            dma((6,)),
            dma((2 * layers * 3,)),
            dma((layers * 3,)),
            dma((layers * 2,)),
            dma((4,)),
            dma((layers * 8,)),
            dma((layers * 8,)),
            dma((layers * 8,)),
            dma((8,)),
            dma((8,)),
            dma((layers,)),
            dma((layers,)),
        ],
        compiler_params=pltpu.CompilerParams(
            collective_id=0, has_side_effects=True, vmem_limit_bytes=60 * 1024 * 1024
        ),
    )(x, gain.reshape(-1, 128), codes, scales, outer.reshape(1, -1), down.T, up, target)
    return kv, loss.reshape(())


def solution(mesh):
    placed = (
        P(("grp", "fsdp"), None),
        P(),
        P("fsdp", None),
        P("fsdp", None),
        P("fsdp"),
        P(),
        P(),
        P(("grp", "fsdp"), None),
    )
    return jax.shard_map(
        functools.partial(per_device, mesh.shape["fsdp"]),
        mesh=mesh,
        in_specs=placed,
        out_specs=(P(("grp", "fsdp"), None), P()),
        check_vma=False,
    )
```

profile of v0, /device:TPU:0, one launch (start us, length us, event | category | flops | bytes accessed | tf_op | source)
XLA Modules:
  0.0 89.9 jit_solution(4152651085852061197)
XLA Ops:
  0.6 85.3 %shard_map.95 = (bf16[512,1024]{1,0:T(8,128)(2,1)}, f32[1,1]{1,0:T(1,128)}) custom-call(bf16[512,8192]{1,0:T(8,128)(2,1)} %x_hbm.1, bf16[64,128]{1,0:T(8,128)(2,1)} %bitcast.5, s32[1024,256]{1,0:T(8,128)} %codes_ref.1, s32[32,128]{1,0:T(8,128)} %scales_ref.1, s32[1,64]{1,0:T(1,128)} %bitcast.6, bf16[64,8192]{1,0:T(8,128)(2,1)} %bitcast.4, ...), custom_call_target="tpu_custom_call" | custom-call | tf_op jit(solution)/shard_map/pallas_call | solution.py:546
  85.9 2.3 %copy.12 = bf16[512,1024]{1,0:T(8,128)(2,1)} copy(bf16[512,1024]{1,0:T(8,128)(2,1)} %get-tuple-element.8) | data formatting | bytes 2097152
where the time goes:
time: 90.1 us; the launch traced here: 89.9 us
  Pallas kernels  85.3 us (95%)
  between operations  2.33 us (3%)
  local copies, waits for them, and re-layouts  2.26 us (3%)
    pallas_call x1, Pallas kernels, per_device(): pl.pallas_call(functools.partial(kernel, layers), out_shape=(jax.ShapeDty...  85.3 us
    unnamed x1, local copies, waits for them, and re-layouts  2.26 us

commit v1 on v0

v1 whole, which is shorter than its diff:
```python
import functools

import jax
import jax.numpy as jnp
from jax import lax
from jax.experimental import pallas as pl
from jax.experimental.pallas import tpu as pltpu
from jax.sharding import PartitionSpec as P

adapter_scale = 0.25
epsilon = 1e-06
nf4_levels = (
    -1.0,
    -0.6961928009986877,
    -0.5250730514526367,
    -0.39491748809814453,
    -0.28444138169288635,
    -0.18477343022823334,
    -0.09105003625154495,
    0.0,
    0.07958029955625534,
    0.16093020141124725,
    0.24611230194568634,
    0.33791524171066284,
    0.44070982933044434,
    0.5626170039176941,
    0.7229568362236023,
    1.0,
)
MESH = pl.DeviceIdType.MESH


def nibble_levels(words, plane):
    values = [jnp.float32(level) for level in nf4_levels]
    for bit in range(4):
        is_set = jnp.bitwise_and(words, 1 << (4 * plane + bit)) != 0
        values = [
            jnp.where(is_set, values[2 * i + 1], values[2 * i])
            for i in range(len(values) // 2)
        ]
    return values[0]


def plan(layers, pieces, groups):
    by_z = max(pieces // 2, pieces * 13 // 16)
    by_y = pieces // 2
    own_y = max(pieces // 2, pieces * 14 // 16)
    early = min(3, own_y)
    y_lag, x_lag = 3, 3
    lag = y_lag + x_lag
    group = pieces // groups
    slots = (layers - 1) * by_z
    spare = by_z - by_y
    ready = max(by_z, by_y + lag)
    per = -(-2 * groups // by_z)

    def own_slot(o):
        if o < early:
            return o - early
        return (o - early) // spare * by_z + by_y + (o - early) % spare

    last = (layers - 2) * by_z
    total = max(slots, last + by_y + lag, own_slot(own_y - 1) + y_lag + 1)
    total = max(total, (layers - 3) * by_z + ready + -(-2 * groups // per))

    def seen(kind, i):
        twin = pieces - 1 - i
        if kind == 0:
            return ready
        if kind == 1:
            return own_slot(i) + y_lag if i < own_y else own_slot(twin) + lag
        if kind == 2:
            return last + (i if i < by_z else twin + lag)
        return last + (i + y_lag if i < by_y else twin + lag)

    items = []
    for kind in range(4):
        for g in range(groups):
            when = max(seen(kind, i) for i in range(g * group, (g + 1) * group))
            items.append((when + 2, kind, g))
    items.sort()
    extras, tail, slot = [], [], ready + 9
    for when, kind, g in items:
        slot = max(slot, when)
        if slot < total:
            extras.append((slot, kind, g))
            slot += 1
        else:
            tail.append((kind, g))
    return dict(
        by_z=by_z,
        by_y=by_y,
        own_y=own_y,
        early=early,
        y_lag=y_lag,
        lag=lag,
        group=group,
        slots=slots,
        spare=spare,
        ready=ready,
        per=per,
        total=total,
        extras=extras,
        tail=tail,
    )


def kernel(
    layers,
    pieces,
    groups,
    x_hbm,
    gain_hbm,
    codes_hbm,
    scales_hbm,
    outer_hbm,
    down_hbm,
    up_hbm,
    target_hbm,
    out_ref,
    loss_ref,
    x_ref,
    weight_ref,
    acc_ref,
    target_ref,
    down_ref,
    up_ref,
    gain_ref,
    codes_ref,
    scales_ref,
    outer_ref,
    spread_ref,
    scale_ref,
    wide_gain_ref,
    low_ref,
    plane_ref,
    line_ref,
    local_sem,
    z_send,
    x_send,
    y_send,
    core_send,
    link_recv,
    core_recv,
    plane_send,
    plane_recv,
    line_send,
    line_recv,
):
    g = lax.axis_index("grp")
    f = lax.axis_index("fsdp")
    cx, cc = g // 2, g % 2
    cl, cy = f // 2, f % 2
    tokens, width = x_ref.shape
    columns = acc_ref.shape[1]
    rows = codes_ref.shape[0]
    high = rows // 2 // pieces
    p = plan(layers, pieces, groups)
    by_z, by_y, own_y, early = p["by_z"], p["by_y"], p["own_y"], p["early"]
    y_lag, lag, group, spare = p["y_lag"], p["lag"], p["group"], p["spare"]
    slots, ready = p["slots"], p["ready"]

    sibling = (cx * 2 + 1 - cc, f)
    x_peer = ((1 - cx) * 2 + cc, f)
    y_peer = (g, cl * 2 + 1 - cy)

    def z_peer(step):
        return (g, (cl + step) * 2 + cy)

    def inside(layer):
        return (layer >= 0) & (layer < layers)

    barrier = pltpu.get_barrier_semaphore()
    for peer in (x_peer, y_peer, sibling):
        pl.semaphore_signal(barrier, inc=1, device_id=peer, device_id_type=MESH)
    for step in (-1, 1):

        @pl.when(inside(cl + step))
        def _():
            pl.semaphore_signal(barrier, inc=1, device_id=z_peer(step), device_id_type=MESH)

    part = tokens // 4
    scales_copy = pltpu.make_async_copy(scales_hbm, scales_ref, local_sem.at[6])
    outer_copy = pltpu.make_async_copy(outer_hbm, outer_ref, local_sem.at[7])
    codes_copy = pltpu.make_async_copy(codes_hbm, codes_ref, local_sem.at[8])
    gain_copy = pltpu.make_async_copy(gain_hbm, gain_ref, local_sem.at[9])
    up_copy = pltpu.make_async_copy(up_hbm, up_ref, local_sem.at[10])
    target_copy = pltpu.make_async_copy(target_hbm, target_ref, local_sem.at[4])
    down_copy = pltpu.make_async_copy(down_hbm, down_ref, local_sem.at[5])

    def x_copy(i):
        at = pl.ds(pl.multiple_of(i * part, part), part)
        return pltpu.make_async_copy(x_hbm.at[at], x_ref.at[at], local_sem.at[i])

    scales_copy.start()
    outer_copy.start()
    codes_copy.start()
    gain_copy.start()
    for i in range(4):
        x_copy(i).start()
    down_copy.start()
    up_copy.start()
    target_copy.start()

    spot = (cx * 2 + cc) * 2 + cy

    def plane_peer(i):
        to = (spot + i) % 8
        return (to // 2, cl * 2 + to % 2)

    def line_peer(i):
        return (g, (cl + i) % layers * 2 + cy)

    def mirror(px, j):
        return j + px * (pieces - 1 - 2 * j)

    def chunk(layer, y, c, q):
        start = (layer * 2 + y) * rows + (q * 2 + c) * high
        return weight_ref.at[pl.ds(pl.multiple_of(start, high), high)]

    def slot(layer, y, q):
        return (layer * 2 + y) * pieces + q

    def link_copy(layer, y, q, send_sem, peer):
        ref = chunk(layer, y, cc, q)
        return pltpu.make_async_remote_copy(
            src_ref=ref,
            dst_ref=ref,
            send_sem=send_sem,
            recv_sem=link_recv.at[slot(layer, y, q)],
            device_id=peer,
            device_id_type=MESH,
        )

    def z_copy(layer, j, step):
        sem = z_send.at[(1 + step) // 2 * layers + layer]
        return link_copy(layer, cy, mirror(cx, j), sem, z_peer(step))

    def x_piece(layer, y, j):
        return link_copy(layer, y, mirror(cx, j), x_send.at[layer], x_peer)

    def y_piece(layer, j):
        return link_copy(layer, cy, mirror(cx, j), y_send.at[layer], y_peer)

    def core_copy(layer, y, q):
        ref = chunk(layer, y, cc, q)
        return pltpu.make_async_remote_copy(
            src_ref=ref,
            dst_ref=ref,
            send_sem=core_send.at[layer * 2 + y],
            recv_sem=core_recv.at[(layer * 2 + y) * groups + q // group],
            device_id=sibling,
            device_id_type=MESH,
        )

    def landed(ref, sem):
        pltpu.make_async_copy(ref, ref, sem).wait()

    def arrived(layer, y, q):
        landed(chunk(layer, y, cc, q), link_recv.at[slot(layer, y, q)])

    def some_rows(count):
        return weight_ref.at[pl.ds(0, count * high)]

    deep = lax.broadcasted_iota(jnp.int32, spread_ref.shape, 0)
    wide = lax.broadcasted_iota(jnp.int32, spread_ref.shape, 1)
    spread_ref[...] = jnp.where(
        (deep % 128) * 4 + deep // 128 == wide, 1.0, 0.0
    ).astype(jnp.bfloat16)

    words = codes_ref.shape[1]
    lanes = scales_ref.shape[1]
    per_row = scales_ref.shape[0] * lanes // rows
    line = rows // scales_ref.shape[0]
    row = lax.broadcasted_iota(jnp.int32, (rows, lanes), 0)
    lane = lax.broadcasted_iota(jnp.int32, (rows, lanes), 1)
    mine = lane // per_row == row % line
    place = lax.broadcasted_iota(jnp.int32, (lanes, words), 0)
    word = lax.broadcasted_iota(jnp.int32, (lanes, words), 1)
    run = words // (4 * per_row)
    code = jnp.zeros((rows, words), jnp.float32)
    scales_copy.wait()
    scale_words = jnp.concatenate(
        [
            jnp.broadcast_to(scales_ref[pl.ds(i, 1), :], (line, lanes))
            for i in range(scales_ref.shape[0])
        ],
        axis=0,
    )
    for byte in range(4):
        value = jnp.bitwise_and(jnp.right_shift(scale_words, 8 * byte), 255)
        value = jnp.where(mine, value.astype(jnp.float32), 0.0).astype(jnp.bfloat16)
        pick = (place % per_row == word // (4 * run)) & ((word // run) % 4 == byte)
        code += jnp.dot(
            value,
            jnp.where(pick, 1.0, 0.0).astype(jnp.bfloat16),
            preferred_element_type=jnp.float32,
        )
    outer_copy.wait()
    outer_count = outer_ref.shape[1]
    outer_rows = rows // outer_count
    outer_row = lax.broadcasted_iota(jnp.int32, (rows, outer_count), 0)
    outer_lane = lax.broadcasted_iota(jnp.int32, (rows, outer_count), 1)
    second = jnp.sum(
        jnp.where(
            outer_row // outer_rows == outer_lane, outer_ref[...].astype(jnp.float32), 0.0
        ),
        axis=1,
        keepdims=True,
    )
    second = jnp.exp2(second / 128.0 - 6.0)
    scale_ref[...] = (code + 0.5) / 256.0 * second

    def decode(c, index):
        starts = [
            pl.multiple_of(((index * group + i) * 2 + c) * high, high) for i in range(group)
        ]
        for h in range(words // 128):
            span = pl.ds(h * 128, 128)
            code_words = jnp.concatenate([codes_ref[pl.ds(s, high), span] for s in starts])
            scale = jnp.concatenate([scale_ref[pl.ds(s, high), span] for s in starts])
            planes = [
                (nibble_levels(code_words, plane) * scale).astype(jnp.bfloat16)
                for plane in range(4)
            ]
            ordered = jnp.dot(
                jnp.concatenate(planes, axis=1),
                spread_ref[...],
                preferred_element_type=jnp.float32,
            ).astype(jnp.bfloat16)
            for i, s in enumerate(starts):
                weight_ref[
                    pl.ds(pl.multiple_of(f * rows + s, high), high), pl.ds(h * 512, 512)
                ] = ordered[i * high : (i + 1) * high]

    def turned(index):
        return index + cx * (groups - 1 - 2 * index)

    def own_sends(index):
        for i in range(group):
            j = index * group + i
            for step in (-1, 1):

                @pl.when(inside(cl + step) & (j < by_z))
                def _():
                    z_copy(cl, j, step).start()

            pl.when(j < early)(lambda: y_piece(cl, j).start())

    codes_copy.wait()
    decode(cc, turned(0))
    neighbours = 3 + jnp.where(cl > 0, 1, 0) + jnp.where(cl < layers - 1, 1, 0)
    pl.semaphore_wait(barrier, neighbours)
    own_sends(0)

    def rest(index, carry):
        decode(cc, turned(index))
        own_sends(index)
        return carry

    lax.fori_loop(1, groups, rest, 0)
    gain_copy.wait()
    wide_gain_ref[...] = gain_ref[...].astype(jnp.float32)

    block = min(16, part)
    blocks = tokens // block
    tile = min(1024, width)

    def normalize(i):
        pl.when(i % (blocks // 4) == 0)(lambda: x_copy(i // (blocks // 4)).wait())
        at = pl.ds(pl.multiple_of(i * block, block), block)
        total = jnp.zeros((block, 128), jnp.float32)
        for t in range(width // tile):
            v = x_ref[at, pl.ds(t * tile, tile)].astype(jnp.float32)
            v = v * v
            for k in range(tile // 128):
                total += v[:, k * 128 : (k + 1) * 128]
        inverse = lax.rsqrt(jnp.sum(total, axis=1, keepdims=True) / width + epsilon)
        for t in range(width // 128):
            span = pl.ds(t * 128, 128)
            v = x_ref[at, span].astype(jnp.float32)
            x_ref[at, span] = (v * inverse * wide_gain_ref[pl.ds(t, 1), :]).astype(jnp.bfloat16)

    def adapter(step):
        at = pl.ds(pl.multiple_of(step * (width // 8), width // 8), width // 8)
        partial = lax.dot_general(
            x_ref[:, at],
            down_ref[:, at],
            (((1,), (1,)), ((), ())),
            preferred_element_type=jnp.float32,
        )

        @pl.when(step == 0)
        def _():
            low_ref[...] = partial

        @pl.when(step > 0)
        def _():
            low_ref[...] += partial

    def adapter_up():
        up_copy.wait()

        acc_ref[...] += adapter_scale * jnp.dot(
            low_ref[...].astype(jnp.bfloat16), up_ref[...], preferred_element_type=jnp.float32
        )

    def multiply(layer, y, index, is_own):
        size = rows // groups

        @pl.when(jnp.logical_not(is_own))
        def _():
            landed(some_rows(group), core_recv.at[(layer * 2 + y) * groups + index])

        at = pl.ds(pl.multiple_of((layer * 2 + y) * rows + index * size, size), size)
        acc_ref[...] += jnp.dot(
            x_ref[:, at], weight_ref[at, :], preferred_element_type=jnp.float32
        )

    shorter = jnp.minimum(cl, layers - 1 - cl)
    longer = jnp.where(cl * 2 < layers - 1, 1, -1)

    def layer_of(v):
        near = v <= 2 * shorter
        away = jnp.where(near, (v + 1) // 2, v - shorter)
        side = jnp.where(near & (v % 2 == 0), -longer, longer)
        return jnp.clip(cl + side * away, 0, layers - 1)

    def stage(k):
        k = jnp.maximum(k, 0)
        return lax.div(k, by_z) + 1, lax.rem(k, by_z)

    def z_event(s, j):
        q = mirror(cx, j)
        for step in (-1, 1):
            layer = cl + step * s

            @pl.when(inside(layer))
            def _():
                arrived(layer, cy, q)
                pl.when(inside(cl - step))(lambda: z_copy(layer, j, -step).start())
                core_copy(layer, cy, q).start()

    def own_index(v, j):
        return early + (v - 1) * spare + j - by_y

    def send_event(v, j):
        layer = layer_of(v)
        pl.when(j < pieces - by_z)(lambda: x_piece(layer, cy, j).start())
        pl.when(j < by_y)(lambda: y_piece(layer, j).start())
        o = own_index(v, j)
        pl.when((j >= by_y) & (o < own_y))(lambda: y_piece(cl, o).start())

    def y_event(k):
        v, j = stage(k)
        o = jnp.where(k < 0, k + early, own_index(v, j))
        moving = (k >= 0) & (j < by_y)
        layer = jnp.where(moving, layer_of(v), cl)
        i = jnp.where(moving, j, o)

        @pl.when(moving | (o < own_y))
        def _():
            q = mirror(cx, i)
            arrived(layer, 1 - cy, q)
            pl.when(moving | (o < pieces - own_y))(
                lambda: x_piece(layer, 1 - cy, i).start()
            )
            core_copy(layer, 1 - cy, q).start()

    def x_event(k):
        v, j = stage(k)
        moving = (k >= 0) & (j < by_y)
        o = k + early
        layer = jnp.where(k < 0, cl, layer_of(v))
        i = jnp.where(k < 0, o, j)
        q = mirror(1 - cx, i)

        @pl.when((k >= 0) & (j < pieces - by_z))
        def _():
            arrived(layer, cy, q)
            core_copy(layer, cy, q).start()

        @pl.when(moving | ((k < 0) & (o < pieces - own_y)))
        def _():
            arrived(layer, 1 - cy, q)
            core_copy(layer, 1 - cy, q).start()

    first = ready - 1
    each = -(-blocks // first)

    def early_work(k):
        def some(i, carry):
            normalize(i)
            return carry

        lax.fori_loop(jnp.minimum(k * each, blocks), jnp.minimum((k + 1) * each, blocks), some, 0)
        often = first // groups
        pl.when((lax.rem(k, often) == 0) & (k < groups * often))(
            lambda: decode(1 - cc, lax.div(k, often))
        )

        @pl.when(k == first - 1)
        def _():
            acc_ref[...] = jnp.zeros(acc_ref.shape, jnp.float32)
            down_copy.wait()

    def extra_of(kind):
        layer = jnp.where(kind < 2, cl, layer_of(layers - 1))
        y = jnp.where(kind % 2 == 0, cy, 1 - cy)
        return layer, y

    def late_work(k):
        past = k - ready
        v, j = stage(past)
        for i in range(p["per"]):
            index = j * p["per"] + i

            @pl.when((v < layers - 1) & (index < 2 * groups))
            def _():
                y = jnp.where(index < groups, cy, 1 - cy)
                multiply(layer_of(v), y, turned(index % groups), False)

        pl.when(past < 8)(lambda: adapter(past))
        pl.when(past == 8)(adapter_up)

        @pl.when(past > 8)
        def _():
            kind, index = jnp.int32(-1), jnp.int32(0)
            for when, a, b in p["extras"]:
                kind = jnp.where(k == when, a, kind)
                index = jnp.where(k == when, b, index)

            @pl.when(kind >= 0)
            def _():
                layer, y = extra_of(kind)
                multiply(layer, y, turned(index), kind == 0)

    def one_slot(k, carry):
        @pl.when(k < slots)
        def _():
            v, j = stage(k)
            z_event(v, j)
            send_event(v, j)

        pl.when(k >= y_lag - early)(lambda: y_event(k - y_lag))
        pl.when(k >= lag - early)(lambda: x_event(k - lag))
        pl.when(k < first)(lambda: early_work(k))
        pl.when(k >= ready)(lambda: late_work(k))
        return carry

    lax.fori_loop(0, p["total"], one_slot, 0)
    for kind, index in p["tail"]:
        layer, y = extra_of(jnp.int32(kind))
        multiply(layer, y, turned(index), kind == 0)

    target_copy.wait()
    plane_ref[spot] = jnp.zeros((8, 128), jnp.float32)

    def finish(i, carry):
        at = pl.ds(pl.multiple_of(i * block, block), block)
        exact = acc_ref[at, :]
        out_ref[at, :] = exact.astype(jnp.bfloat16)
        error = exact - target_ref[at, :].astype(jnp.float32)
        error = error * error
        total = jnp.zeros((block, 128), jnp.float32)
        for k in range(columns // 128):
            total += error[:, k * 128 : (k + 1) * 128]
        for k in range(block // 8):
            plane_ref[spot] += total[k * 8 : (k + 1) * 8]
        return carry

    lax.fori_loop(0, tokens // block, finish, 0)

    def plane_copy(i):
        return pltpu.make_async_remote_copy(
            src_ref=plane_ref.at[spot],
            dst_ref=plane_ref.at[spot],
            send_sem=plane_send.at[i],
            recv_sem=plane_recv.at[spot],
            device_id=plane_peer(i),
            device_id_type=MESH,
        )

    def line_copy(i):
        return pltpu.make_async_remote_copy(
            src_ref=line_ref.at[cl],
            dst_ref=line_ref.at[cl],
            send_sem=line_send.at[i],
            recv_sem=line_recv.at[cl],
            device_id=line_peer(i),
            device_id_type=MESH,
        )

    for i in range(1, 8):
        plane_copy(i).start()

    def sent(layer, carry):
        for step in (-1, 1):

            @pl.when(inside(cl + step) & ((cl - layer) * step >= 0))
            def _():
                landed(some_rows(by_z), z_send.at[(1 + step) // 2 * layers + layer])

        @pl.when(layer == cl)
        def _():
            landed(some_rows(own_y), y_send.at[layer])
            landed(some_rows(pieces - own_y), x_send.at[layer])

        @pl.when(layer != cl)
        def _():
            landed(some_rows(by_y), y_send.at[layer])
            landed(some_rows(pieces - by_z + by_y), x_send.at[layer])
            landed(some_rows(pieces), core_send.at[layer * 2 + cy])

        landed(some_rows(pieces), core_send.at[layer * 2 + 1 - cy])
        return carry

    lax.fori_loop(0, layers, sent, 0)
    for i in range(1, 8):
        source = (spot + i) % 8
        landed(plane_ref.at[source], plane_recv.at[source])
    line_ref[cl] = jnp.sum(plane_ref[...], axis=0)

    def to_line(i, carry):
        line_copy(i).start()
        return carry

    def from_line(i, carry):
        source = (cl + i) % layers
        landed(line_ref.at[source], line_recv.at[source])
        line_copy(i).wait_send()
        return carry

    lax.fori_loop(1, layers, to_line, 0)
    for i in range(1, 8):
        plane_copy(i).wait_send()
    lax.fori_loop(1, layers, from_line, 0)
    loss_ref[0, 0] = jnp.sum(line_ref[...]) / (tokens * layers * 2 * columns)


def per_device(fsdp, x, gain, codes, scales, outer, down, up, target):
    tokens, width = x.shape
    columns = up.shape[1]
    rows = codes.shape[0]
    layers = fsdp // 2
    pieces = rows // 2 // max(16, rows // 32)
    groups = min(4, rows // 128)
    hbm = pl.BlockSpec(memory_space=pltpu.HBM)
    dma = pltpu.SemaphoreType.DMA
    gain = gain.reshape(-1, 128)
    outer = outer.reshape(1, -1)
    operands = (x, gain, codes, scales, outer, down.T, up, target)
    operands = [pltpu.with_memory_space_constraint(a, pltpu.HBM) for a in operands]
    kv, loss = pl.pallas_call(
        functools.partial(kernel, layers, pieces, groups),
        out_shape=(
            jax.ShapeDtypeStruct((tokens, columns), jnp.bfloat16),
            jax.ShapeDtypeStruct((1, 1), jnp.float32),
        ),
        in_specs=[hbm] * 8,
        out_specs=(
            pl.BlockSpec(memory_space=pltpu.VMEM),
            pl.BlockSpec(memory_space=pltpu.SMEM),
        ),
        scratch_shapes=[
            pltpu.VMEM((tokens, width), jnp.bfloat16),
            pltpu.VMEM((width, columns), jnp.bfloat16),
            pltpu.VMEM((tokens, columns), jnp.float32),
            pltpu.VMEM((tokens, columns), jnp.bfloat16),
            pltpu.VMEM(down.shape[::-1], jnp.bfloat16),
            pltpu.VMEM(up.shape, jnp.bfloat16),
            pltpu.VMEM(gain.shape, jnp.bfloat16),
            pltpu.VMEM(codes.shape, jnp.int32),
            pltpu.VMEM(scales.shape, jnp.int32),
            pltpu.VMEM(outer.shape, jnp.int32),
            pltpu.VMEM((512, 512), jnp.bfloat16),
            pltpu.VMEM(codes.shape, jnp.float32),
            pltpu.VMEM((width // 128, 128), jnp.float32),
            pltpu.VMEM((tokens, down.shape[1]), jnp.float32),
            pltpu.VMEM((8, 8, 128), jnp.float32),
            pltpu.VMEM((layers, 8, 128), jnp.float32),
            dma((11,)),
            dma((2 * layers,)),
            dma((layers,)),
            dma((layers,)),
            dma((2 * layers,)),
            dma((layers * 2 * pieces,)),
            dma((layers * 2 * groups,)),
            dma((8,)),
            dma((8,)),
            dma((layers,)),
            dma((layers,)),
        ],
        compiler_params=pltpu.CompilerParams(
            collective_id=0, has_side_effects=True, vmem_limit_bytes=40 * 1024 * 1024
        ),
    )(*operands)
    return kv, loss.reshape(())


def solution(mesh):
    placed = (
        P(("grp", "fsdp"), None),
        P(),
        P("fsdp", None),
        P("fsdp", None),
        P("fsdp"),
        P(),
        P(),
        P(("grp", "fsdp"), None),
    )
    return jax.shard_map(
        functools.partial(per_device, mesh.shape["fsdp"]),
        mesh=mesh,
        in_specs=placed,
        out_specs=(P(("grp", "fsdp"), None), P()),
        check_vma=False,
    )
```

time: 90.1 us -> 79.7 us (0.88)
  Pallas kernels: 85.3 us -> 76.1 us
  local copies, waits for them, and re-layouts: 2.26 us -> 0.97 us
    pallas_call x1, Pallas kernels: 85.3 us -> 76.1 us  [per_device(): pl.pallas_call(functools.partial(kernel, layers, pieces, groups), out_sha...]
    unnamed x1, local copies, waits for them, and re-layouts: 2.26 us -> 0.97 us
where the time goes in v1:
time: 79.7 us; the launch traced here: 79.4 us
  Pallas kernels  76.1 us (95%)
  between operations  2.33 us (3%)
  local copies, waits for them, and re-layouts  0.97 us (1%)
    pallas_call x1, Pallas kernels, per_device(): pl.pallas_call(functools.partial(kernel, layers, pieces, groups), out_sha...  76.1 us

profile of v1, /device:TPU:0, one launch (start us, length us, event | category | flops | bytes accessed | tf_op | source)
XLA Modules:
  0.0 79.4 jit_solution(15373854315289001449)
XLA Ops:
  0.6 76.1 %shard_map.95 = (bf16[512,1024]{1,0:T(8,128)(2,1)S(1)}, f32[1,1]{1,0:T(1,128)}) custom-call(bf16[512,8192]{1,0:T(8,128)(2,1)} %x_hbm.1, bf16[64,128]{1,0:T(8,128)(2,1)} %bitcast.5, s32[1024,256]{1,0:T(8,128)} %codes_hbm.1, s32[32,128]{1,0:T(8,128)} %scales_hbm.1, s32[1,64]{1,0:T(1,128)} %bitcast.6, bf16[64,8192]{1,0:T(8,128)(2,1)} %bitcast.4, ...), custom_call_target="tpu_custom_call" | custom-call | tf_op jit(solution)/shard_map/pallas_call | solution.py:654
  76.8 1.0 %copy.12 = bf16[512,1024]{1,0:T(8,128)(2,1)} copy(bf16[512,1024]{1,0:T(8,128)(2,1)S(1)} %get-tuple-element.8) | data formatting | bytes 2097152

commit v2 on v1

--- a/solution.py
+++ b/solution.py
@@ -28,6 +28,7 @@
     1.0,
 )
 MESH = pl.DeviceIdType.MESH
+FAR, OWN, EARLY, YLAG, XLAG = 0, 14, 4, 4, 3
 
 
 def nibble_levels(words, plane):
@@ -41,64 +42,97 @@
     return values[0]
 
 
-def plan(layers, pieces, groups):
+def plan(layers, pieces, groups, blocks):
     by_z = max(pieces // 2, pieces * 13 // 16)
+    far = max(pieces // 2, by_z - pieces // 16 * FAR)
     by_y = pieces // 2
-    own_y = max(pieces // 2, pieces * 14 // 16)
-    early = min(3, own_y)
-    y_lag, x_lag = 3, 3
+    own_y = pieces * OWN // 16
+    early = min(EARLY, own_y)
+    y_lag, x_lag = YLAG, XLAG
     lag = y_lag + x_lag
     group = pieces // groups
-    slots = (layers - 1) * by_z
     spare = by_z - by_y
+    turn = (layers - 3) * by_z + by_y
+    slots = turn + by_z + far - by_y
     ready = max(by_z, by_y + lag)
     per = -(-2 * groups // by_z)
+    each = -(-blocks // (ready - 1))
+    normal = -(-blocks // each)
 
     def own_slot(o):
         if o < early:
             return o - early
-        return (o - early) // spare * by_z + by_y + (o - early) % spare
-
-    last = (layers - 2) * by_z
-    total = max(slots, last + by_y + lag, own_slot(own_y - 1) + y_lag + 1)
-    total = max(total, (layers - 3) * by_z + ready + -(-2 * groups // per))
+        o -= early
+        if o < (layers - 3) * spare:
+            return o // spare * by_z + by_y + o % spare
+        return turn + by_y + o - (layers - 3) * spare
+
+    def z_slot(hop, i):
+        if hop == layers - 1:
+            return turn + i if i < by_y else turn + by_z + i - by_y
+        if hop == layers - 2:
+            return (layers - 3) * by_z + i if i < by_y else turn + i
+        return (hop - 1) * by_z + i
+
+    def send_slot(v, i):
+        return turn + i if v == layers - 1 else (v - 1) * by_z + i
+
+    last_x = turn + by_y + y_lag
+    total = max(slots, last_x + x_lag + pieces - far, own_slot(own_y - 1) + y_lag + 1)
+    total = max(total, (layers - 4) * by_z + ready + -(-2 * groups // per))
 
     def seen(kind, i):
         twin = pieces - 1 - i
         if kind == 0:
-            return ready
+            return normal - 1
         if kind == 1:
             return own_slot(i) + y_lag if i < own_y else own_slot(twin) + lag
-        if kind == 2:
-            return last + (i if i < by_z else twin + lag)
-        return last + (i + y_lag if i < by_y else twin + lag)
+        v = layers - 1 - (kind - 2) // 2
+        if kind % 2 == 0:
+            when = 0
+            for shorter in range((layers + 1) // 2):
+                hop = (v + 1) // 2 if v <= 2 * shorter else v - shorter
+                count = far if hop == layers - 1 else by_z
+                over = last_x + x_lag + twin if v == layers - 1 else send_slot(v, twin) + lag
+                when = max(when, z_slot(hop, i) if i < count else over)
+            return when
+        return send_slot(v, i) + y_lag if i < by_y else send_slot(v, twin) + lag
 
     items = []
-    for kind in range(4):
+    for kind in range(6):
         for g in range(groups):
             when = max(seen(kind, i) for i in range(g * group, (g + 1) * group))
-            items.append((when + 2, kind, g))
+            items.append((max(when + 2, normal), kind, g))
     items.sort()
-    extras, tail, slot = [], [], ready + 9
+    extras, tail = [], []
+    taken = {}
     for when, kind, g in items:
-        slot = max(slot, when)
-        if slot < total:
-            extras.append((slot, kind, g))
+        slot = when
+        while ready <= slot < ready + 9 or taken.get(slot, 0) >= (1 if slot < turn + by_y else 2):
             slot += 1
+        taken[slot] = taken.get(slot, 0) + 1
+        if slot < slots - 1:
+            extras.append((slot, taken[slot], kind, g))
         else:
             tail.append((kind, g))
     return dict(
         by_z=by_z,
+        far=far,
         by_y=by_y,
         own_y=own_y,
         early=early,
         y_lag=y_lag,
         lag=lag,
         group=group,
+        turn=turn,
+        last_x=last_x,
+        x_lag=x_lag,
         slots=slots,
         spare=spare,
         ready=ready,
         per=per,
+        each=each,
+        normal=normal,
         total=total,
         extras=extras,
         tail=tail,
@@ -130,11 +164,12 @@
     scales_ref,
     outer_ref,
     spread_ref,
+    pick_ref,
     scale_ref,
     wide_gain_ref,
     low_ref,
-    plane_ref,
-    line_ref,
+    share_ref,
+    losses_ref,
     local_sem,
     z_send,
     x_send,
@@ -142,10 +177,7 @@
     core_send,
     link_recv,
     core_recv,
-    plane_send,
-    plane_recv,
-    line_send,
-    line_recv,
+    loss_sem,
 ):
     g = lax.axis_index("grp")
     f = lax.axis_index("fsdp")
@@ -155,10 +187,12 @@
     columns = acc_ref.shape[1]
     rows = codes_ref.shape[0]
     high = rows // 2 // pieces
-    p = plan(layers, pieces, groups)
+    block = min(16, tokens // 4)
+    blocks = tokens // block
+    p = plan(layers, pieces, groups, blocks)
     by_z, by_y, own_y, early = p["by_z"], p["by_y"], p["own_y"], p["early"]
     y_lag, lag, group, spare = p["y_lag"], p["lag"], p["group"], p["spare"]
-    slots, ready = p["slots"], p["ready"]
+    slots, ready, far, turn = p["slots"], p["ready"], p["far"], p["turn"]
 
     sibling = (cx * 2 + 1 - cc, f)
     x_peer = ((1 - cx) * 2 + cc, f)
@@ -166,6 +200,9 @@
 
     def z_peer(step):
         return (g, (cl + step) * 2 + cy)
+
+    def by_hop(h):
+        return jnp.where(h == layers - 1, far, by_z)
 
     def inside(layer):
         return (layer >= 0) & (layer < layers)
@@ -202,15 +239,6 @@
     up_copy.start()
     target_copy.start()
 
-    spot = (cx * 2 + cc) * 2 + cy
-
-    def plane_peer(i):
-        to = (spot + i) % 8
-        return (to // 2, cl * 2 + to % 2)
-
-    def line_peer(i):
-        return (g, (cl + i) % layers * 2 + cy)
-
     def mirror(px, j):
         return j + px * (pieces - 1 - 2 * j)
 
@@ -272,44 +300,43 @@
     lanes = scales_ref.shape[1]
     per_row = scales_ref.shape[0] * lanes // rows
     line = rows // scales_ref.shape[0]
-    row = lax.broadcasted_iota(jnp.int32, (rows, lanes), 0)
-    lane = lax.broadcasted_iota(jnp.int32, (rows, lanes), 1)
+    run = words // (4 * per_row)
+    bunch = rows // groups
+    lines = scales_ref.shape[0] // groups
+    place = lax.broadcasted_iota(jnp.int32, pick_ref.shape, 0)
+    word = lax.broadcasted_iota(jnp.int32, pick_ref.shape, 1)
+    pick = (place % per_row == word // (4 * run)) & ((word // run) % 4 == place // lanes)
+    pick_ref[...] = jnp.where(pick, 1.0, 0.0).astype(jnp.bfloat16)
+    row = lax.broadcasted_iota(jnp.int32, (bunch, lanes), 0)
+    lane = lax.broadcasted_iota(jnp.int32, (bunch, lanes), 1)
     mine = lane // per_row == row % line
-    place = lax.broadcasted_iota(jnp.int32, (lanes, words), 0)
-    word = lax.broadcasted_iota(jnp.int32, (lanes, words), 1)
-    run = words // (4 * per_row)
-    code = jnp.zeros((rows, words), jnp.float32)
-    scales_copy.wait()
-    scale_words = jnp.concatenate(
-        [
-            jnp.broadcast_to(scales_ref[pl.ds(i, 1), :], (line, lanes))
-            for i in range(scales_ref.shape[0])
-        ],
-        axis=0,
-    )
-    for byte in range(4):
-        value = jnp.bitwise_and(jnp.right_shift(scale_words, 8 * byte), 255)
-        value = jnp.where(mine, value.astype(jnp.float32), 0.0).astype(jnp.bfloat16)
-        pick = (place % per_row == word // (4 * run)) & ((word // run) % 4 == byte)
-        code += jnp.dot(
-            value,
-            jnp.where(pick, 1.0, 0.0).astype(jnp.bfloat16),
-            preferred_element_type=jnp.float32,
-        )
-    outer_copy.wait()
     outer_count = outer_ref.shape[1]
     outer_rows = rows // outer_count
-    outer_row = lax.broadcasted_iota(jnp.int32, (rows, outer_count), 0)
-    outer_lane = lax.broadcasted_iota(jnp.int32, (rows, outer_count), 1)
-    second = jnp.sum(
-        jnp.where(
-            outer_row // outer_rows == outer_lane, outer_ref[...].astype(jnp.float32), 0.0
-        ),
-        axis=1,
-        keepdims=True,
-    )
-    second = jnp.exp2(second / 128.0 - 6.0)
-    scale_ref[...] = (code + 0.5) / 256.0 * second
+    outer_row = lax.broadcasted_iota(jnp.int32, (bunch, outer_count), 0) // outer_rows
+    outer_lane = lax.broadcasted_iota(jnp.int32, (bunch, outer_count), 1)
+
+    def unpack(index):
+        scale_words = jnp.concatenate(
+            [
+                jnp.broadcast_to(scales_ref[pl.ds(index * lines + i, 1), :], (line, lanes))
+                for i in range(lines)
+            ],
+            axis=0,
+        )
+        values = []
+        for byte in range(4):
+            value = jnp.bitwise_and(jnp.right_shift(scale_words, 8 * byte), 255)
+            values.append(jnp.where(mine, value.astype(jnp.float32), 0.0).astype(jnp.bfloat16))
+        code = jnp.dot(
+            jnp.concatenate(values, axis=1), pick_ref[...], preferred_element_type=jnp.float32
+        )
+        mask = outer_row + index * (bunch // outer_rows) == outer_lane
+        second = jnp.sum(
+            jnp.where(mask, outer_ref[...].astype(jnp.float32), 0.0), axis=1, keepdims=True
+        )
+        second = jnp.exp2(second / 128.0 - 6.0)
+        at = pl.ds(pl.multiple_of(index * bunch, bunch), bunch)
+        scale_ref[at, :] = (code + 0.5) / 256.0 * second
 
     def decode(c, index):
         starts = [
@@ -341,12 +368,15 @@
             j = index * group + i
             for step in (-1, 1):
 
-                @pl.when(inside(cl + step) & (j < by_z))
+                @pl.when(inside(cl + step) & (j < by_hop(1)))
                 def _():
                     z_copy(cl, j, step).start()
 
             pl.when(j < early)(lambda: y_piece(cl, j).start())
 
+    scales_copy.wait()
+    outer_copy.wait()
+    unpack(turned(0))
     codes_copy.wait()
     decode(cc, turned(0))
     neighbours = 3 + jnp.where(cl > 0, 1, 0) + jnp.where(cl < layers - 1, 1, 0)
@@ -354,6 +384,7 @@
     own_sends(0)
 
     def rest(index, carry):
+        unpack(turned(index))
         decode(cc, turned(index))
         own_sends(index)
         return carry
@@ -362,8 +393,6 @@
     gain_copy.wait()
     wide_gain_ref[...] = gain_ref[...].astype(jnp.float32)
 
-    block = min(16, part)
-    blocks = tokens // block
     tile = min(1024, width)
 
     def normalize(i):
@@ -420,9 +449,12 @@
     shorter = jnp.minimum(cl, layers - 1 - cl)
     longer = jnp.where(cl * 2 < layers - 1, 1, -1)
 
+    def hops_of(v):
+        return jnp.where(v <= 2 * shorter, (v + 1) // 2, v - shorter)
+
     def layer_of(v):
         near = v <= 2 * shorter
-        away = jnp.where(near, (v + 1) // 2, v - shorter)
+        away = hops_of(v)
         side = jnp.where(near & (v % 2 == 0), -longer, longer)
         return jnp.clip(cl + side * away, 0, layers - 1)
 
@@ -430,29 +462,62 @@
         k = jnp.maximum(k, 0)
         return lax.div(k, by_z) + 1, lax.rem(k, by_z)
 
-    def z_event(s, j):
+    def z_stage(k):
+        s, j = stage(k)
+        past = k - turn
+        s = jnp.where(past >= 0, layers - 1, s)
+        j = jnp.where(past >= 0, past, j)
+        second = (past >= by_y) & (past < by_z)
+        s = jnp.where(second, layers - 2, s)
+        j = jnp.where(past >= by_z, past - by_z + by_y, j)
+        return s, j
+
+    def send_stage(k):
+        v, j = stage(k)
+        past = k - turn
+        return jnp.where(past >= 0, layers - 1, v), jnp.where(past >= 0, past, j)
+
+    def held(hop, j):
+        return (hop == layers - 3) & (j >= by_y)
+
+    def z_event(k):
+        s, j = z_stage(k)
         q = mirror(cx, j)
+        late = k - (layers - 3) * by_z
         for step in (-1, 1):
             layer = cl + step * s
 
-            @pl.when(inside(layer))
+            @pl.when(inside(layer) & (j < by_hop(s)))
             def _():
                 arrived(layer, cy, q)
-                pl.when(inside(cl - step))(lambda: z_copy(layer, j, -step).start())
+                go = inside(cl - step) & (j < by_hop(s + 1)) & jnp.logical_not(held(s, j))
+                pl.when(go)(lambda: z_copy(layer, j, -step).start())
                 core_copy(layer, cy, q).start()
 
+            if layers > 3:
+                layer_held = cl + step * (layers - 3)
+                waiting = (late >= by_y) & (late < by_z) & (late < by_hop(layers - 2))
+
+                @pl.when(waiting & inside(layer_held) & inside(cl - step))
+                def _():
+                    z_copy(layer_held, late, -step).start()
+
     def own_index(v, j):
+        v = jnp.minimum(v, layers - 2)
         return early + (v - 1) * spare + j - by_y
 
-    def send_event(v, j):
+    def send_event(k):
+        v, j = send_stage(k)
         layer = layer_of(v)
-        pl.when(j < pieces - by_z)(lambda: x_piece(layer, cy, j).start())
+        pl.when((v < layers - 1) & (j < pieces - by_hop(hops_of(v))))(
+            lambda: x_piece(layer, cy, j).start()
+        )
         pl.when(j < by_y)(lambda: y_piece(layer, j).start())
         o = own_index(v, j)
         pl.when((j >= by_y) & (o < own_y))(lambda: y_piece(cl, o).start())
 
     def y_event(k):
-        v, j = stage(k)
+        v, j = send_stage(k)
         o = jnp.where(k < 0, k + early, own_index(v, j))
         moving = (k >= 0) & (j < by_y)
         layer = jnp.where(moving, layer_of(v), cl)
@@ -468,14 +533,14 @@
             core_copy(layer, 1 - cy, q).start()
 
     def x_event(k):
-        v, j = stage(k)
+        v, j = send_stage(k)
         moving = (k >= 0) & (j < by_y)
         o = k + early
         layer = jnp.where(k < 0, cl, layer_of(v))
         i = jnp.where(k < 0, o, j)
         q = mirror(1 - cx, i)
 
-        @pl.when((k >= 0) & (j < pieces - by_z))
+        @pl.when((k >= 0) & (v < layers - 1) & (j < pieces - by_hop(hops_of(v))))
         def _():
             arrived(layer, cy, q)
             core_copy(layer, cy, q).start()
@@ -485,8 +550,22 @@
             arrived(layer, 1 - cy, q)
             core_copy(layer, 1 - cy, q).start()
 
-    first = ready - 1
-    each = -(-blocks // first)
+    def last_x_event(k):
+        v = layers - 1
+        layer = layer_of(v)
+        count = pieces - by_hop(hops_of(v))
+        j = k - p["last_x"]
+        pl.when((j >= 0) & (j < count))(lambda: x_piece(layer, cy, j).start())
+        i = j - p["x_lag"]
+
+        @pl.when((i >= 0) & (i < count))
+        def _():
+            q = mirror(1 - cx, i)
+            arrived(layer, cy, q)
+            core_copy(layer, cy, q).start()
+
+    each = p["each"]
+    often = max(1, (p["normal"] - 1) // groups)
 
     def early_work(k):
         def some(i, carry):
@@ -494,20 +573,36 @@
             return carry
 
         lax.fori_loop(jnp.minimum(k * each, blocks), jnp.minimum((k + 1) * each, blocks), some, 0)
-        often = first // groups
         pl.when((lax.rem(k, often) == 0) & (k < groups * often))(
             lambda: decode(1 - cc, lax.div(k, often))
         )
 
-        @pl.when(k == first - 1)
+        @pl.when(k == p["normal"] - 1)
         def _():
             acc_ref[...] = jnp.zeros(acc_ref.shape, jnp.float32)
             down_copy.wait()
 
     def extra_of(kind):
-        layer = jnp.where(kind < 2, cl, layer_of(layers - 1))
-        y = jnp.where(kind % 2 == 0, cy, 1 - cy)
+        layer = layer_of(layers - 1 - lax.div(jnp.maximum(kind - 2, 0), 2))
+        layer = jnp.where(kind < 2, cl, layer)
+        y = jnp.where(lax.rem(kind, 2) == 0, cy, 1 - cy)
         return layer, y
+
+    def extra_work(k):
+        for order in (1, 2):
+            chosen = [e for e in p["extras"] if e[1] == order]
+
+            @pl.when(k >= min([e[0] for e in chosen], default=p["total"]))
+            def _():
+                choice = jnp.int32(-1)
+                for when, _, a, b in chosen:
+                    choice = jnp.where(k == when, a * groups + b, choice)
+
+                @pl.when(choice >= 0)
+                def _():
+                    kind, index = lax.div(choice, groups), lax.rem(choice, groups)
+                    layer, y = extra_of(kind)
+                    multiply(layer, y, turned(index), kind == 0)
 
     def late_work(k):
         past = k - ready
@@ -515,37 +610,26 @@
         for i in range(p["per"]):
             index = j * p["per"] + i
 
-            @pl.when((v < layers - 1) & (index < 2 * groups))
+            @pl.when((v < layers - 2) & (index < 2 * groups))
             def _():
                 y = jnp.where(index < groups, cy, 1 - cy)
-                multiply(layer_of(v), y, turned(index % groups), False)
+                multiply(layer_of(v), y, turned(lax.rem(index, groups)), False)
 
         pl.when(past < 8)(lambda: adapter(past))
         pl.when(past == 8)(adapter_up)
 
-        @pl.when(past > 8)
-        def _():
-            kind, index = jnp.int32(-1), jnp.int32(0)
-            for when, a, b in p["extras"]:
-                kind = jnp.where(k == when, a, kind)
-                index = jnp.where(k == when, b, index)
-
-            @pl.when(kind >= 0)
-            def _():
-                layer, y = extra_of(kind)
-                multiply(layer, y, turned(index), kind == 0)
-
     def one_slot(k, carry):
         @pl.when(k < slots)
         def _():
-            v, j = stage(k)
-            z_event(v, j)
-            send_event(v, j)
+            z_event(k)
+            send_event(k)
 
         pl.when(k >= y_lag - early)(lambda: y_event(k - y_lag))
         pl.when(k >= lag - early)(lambda: x_event(k - lag))
-        pl.when(k < first)(lambda: early_work(k))
+        pl.when(k >= p["last_x"])(lambda: last_x_event(k))
+        pl.when(k < p["normal"])(lambda: early_work(k))
         pl.when(k >= ready)(lambda: late_work(k))
+        extra_work(k)
         return carry
 
     lax.fori_loop(0, p["total"], one_slot, 0)
@@ -554,7 +638,7 @@
         multiply(layer, y, turned(index), kind == 0)
 
     target_copy.wait()
-    plane_ref[spot] = jnp.zeros((8, 128), jnp.float32)
+    share_ref[...] = jnp.zeros((8, 128), jnp.float32)
 
     def finish(i, carry):
         at = pl.ds(pl.multiple_of(i * block, block), block)
@@ -566,76 +650,70 @@
         for k in range(columns // 128):
             total += error[:, k * 128 : (k + 1) * 128]
         for k in range(block // 8):
-            plane_ref[spot] += total[k * 8 : (k + 1) * 8]
+            share_ref[...] += total[k * 8 : (k + 1) * 8]
         return carry
 
     lax.fori_loop(0, tokens // block, finish, 0)
 
-    def plane_copy(i):
-        return pltpu.make_async_remote_copy(
-            src_ref=plane_ref.at[spot],
-            dst_ref=plane_ref.at[spot],
-            send_sem=plane_send.at[i],
-            recv_sem=plane_recv.at[spot],
-            device_id=plane_peer(i),
-            device_id_type=MESH,
-        )
-
-    def line_copy(i):
-        return pltpu.make_async_remote_copy(
-            src_ref=line_ref.at[cl],
-            dst_ref=line_ref.at[cl],
-            send_sem=line_send.at[i],
-            recv_sem=line_recv.at[cl],
-            device_id=line_peer(i),
-            device_id_type=MESH,
-        )
-
-    for i in range(1, 8):
-        plane_copy(i).start()
+    fsdp = layers * 2
+    members = 4 * fsdp
+    spot = g * fsdp + f
+    losses_ref[spot] = jnp.sum(share_ref[...], axis=0, keepdims=True)
+
+    def tell(j, carry):
+        to = f + j
+        to = jnp.where(to >= fsdp, to - fsdp, to)
+        for i in range(4):
+
+            @pl.when((i > 0) | (j > 0))
+            def _():
+                pltpu.make_async_remote_copy(
+                    src_ref=losses_ref.at[spot],
+                    dst_ref=losses_ref.at[spot],
+                    send_sem=loss_sem.at[0],
+                    recv_sem=loss_sem.at[1],
+                    device_id=((g + i) % 4, to),
+                    device_id_type=MESH,
+                ).start()
+
+        return carry
+
+    lax.fori_loop(0, fsdp, tell, 0)
 
     def sent(layer, carry):
+        hops = jnp.abs(cl - layer)
         for step in (-1, 1):
 
-            @pl.when(inside(cl + step) & ((cl - layer) * step >= 0))
-            def _():
-                landed(some_rows(by_z), z_send.at[(1 + step) // 2 * layers + layer])
+            for count, test in ((far, hops == layers - 2), (by_z, hops < layers - 2)):
+
+                @pl.when(inside(cl + step) & ((cl - layer) * step >= 0) & test)
+                def _():
+                    landed(some_rows(count), z_send.at[(1 + step) // 2 * layers + layer])
 
         @pl.when(layer == cl)
         def _():
             landed(some_rows(own_y), y_send.at[layer])
-            landed(some_rows(pieces - own_y), x_send.at[layer])
+            if own_y < pieces:
+                landed(some_rows(pieces - own_y), x_send.at[layer])
 
         @pl.when(layer != cl)
         def _():
             landed(some_rows(by_y), y_send.at[layer])
-            landed(some_rows(pieces - by_z + by_y), x_send.at[layer])
+            for count, test in ((far, hops == layers - 1), (by_z, hops < layers - 1)):
+                pl.when(test)(
+                    lambda: landed(some_rows(pieces - count + by_y), x_send.at[layer])
+                )
             landed(some_rows(pieces), core_send.at[layer * 2 + cy])
 
         landed(some_rows(pieces), core_send.at[layer * 2 + 1 - cy])
         return carry
 
     lax.fori_loop(0, layers, sent, 0)
-    for i in range(1, 8):
-        source = (spot + i) % 8
-        landed(plane_ref.at[source], plane_recv.at[source])
-    line_ref[cl] = jnp.sum(plane_ref[...], axis=0)
-
-    def to_line(i, carry):
-        line_copy(i).start()
-        return carry
-
-    def from_line(i, carry):
-        source = (cl + i) % layers
-        landed(line_ref.at[source], line_recv.at[source])
-        line_copy(i).wait_send()
-        return carry
-
-    lax.fori_loop(1, layers, to_line, 0)
-    for i in range(1, 8):
-        plane_copy(i).wait_send()
-    lax.fori_loop(1, layers, from_line, 0)
-    loss_ref[0, 0] = jnp.sum(line_ref[...]) / (tokens * layers * 2 * columns)
+    others = losses_ref.at[pl.ds(0, members - 1)]
+    landed(others, loss_sem.at[1])
+    everyone = jnp.sum(losses_ref[...], axis=0)
+    loss_ref[...] = jnp.sum(everyone, axis=1, keepdims=True) / (tokens * fsdp * columns)
+    landed(others, loss_sem.at[0])
 
 
 def per_device(fsdp, x, gain, codes, scales, outer, down, up, target):
@@ -660,7 +738,7 @@
         in_specs=[hbm] * 8,
         out_specs=(
             pl.BlockSpec(memory_space=pltpu.VMEM),
-            pl.BlockSpec(memory_space=pltpu.SMEM),
+            pl.BlockSpec(memory_space=pltpu.VMEM),
         ),
         scratch_shapes=[
             pltpu.VMEM((tokens, width), jnp.bfloat16),
@@ -674,11 +752,12 @@
             pltpu.VMEM(scales.shape, jnp.int32),
             pltpu.VMEM(outer.shape, jnp.int32),
             pltpu.VMEM((512, 512), jnp.bfloat16),
+            pltpu.VMEM((4 * scales.shape[1], codes.shape[1]), jnp.bfloat16),
             pltpu.VMEM(codes.shape, jnp.float32),
             pltpu.VMEM((width // 128, 128), jnp.float32),
             pltpu.VMEM((tokens, down.shape[1]), jnp.float32),
-            pltpu.VMEM((8, 8, 128), jnp.float32),
-            pltpu.VMEM((layers, 8, 128), jnp.float32),
+            pltpu.VMEM((8, 128), jnp.float32),
+            pltpu.VMEM((4 * fsdp, 1, 128), jnp.float32),
             dma((11,)),
             dma((2 * layers,)),
             dma((layers,)),
@@ -686,10 +765,7 @@
             dma((2 * layers,)),
             dma((layers * 2 * pieces,)),
             dma((layers * 2 * groups,)),
-            dma((8,)),
-            dma((8,)),
-            dma((layers,)),
-            dma((layers,)),
+            dma((2,)),
         ],
         compiler_params=pltpu.CompilerParams(
             collective_id=0, has_side_effects=True, vmem_limit_bytes=40 * 1024 * 1024

time: 79.7 us -> 74.6 us (0.936)
  Pallas kernels: 76.1 us -> 71 us
    pallas_call x1, Pallas kernels: 76.1 us -> 71 us  [per_device(): pl.pallas_call(functools.partial(kernel, layers, pieces, groups), out_sha...]
where the time goes in v2:
time: 74.6 us; the launch traced here: 74.3 us
  Pallas kernels  71 us (95%)
  between operations  2.33 us (3%)
  local copies, waits for them, and re-layouts  0.97 us (1%)
    pallas_call x1, Pallas kernels, per_device(): pl.pallas_call(functools.partial(kernel, layers, pieces, groups), out_sha...  71 us

profile of v2, /device:TPU:0, one launch (start us, length us, event | category | flops | bytes accessed | tf_op | source)
XLA Modules:
  0.0 74.3 jit_solution(10885689482434896946)
XLA Ops:
  0.6 71.0 %shard_map.95 = (bf16[512,1024]{1,0:T(8,128)(2,1)S(1)}, f32[1,1]{1,0:T(1,128)}) custom-call(bf16[512,8192]{1,0:T(8,128)(2,1)} %x_hbm.1, bf16[64,128]{1,0:T(8,128)(2,1)} %bitcast.5, s32[1024,256]{1,0:T(8,128)} %codes_hbm.1, s32[32,128]{1,0:T(8,128)} %scales_hbm.1, s32[1,64]{1,0:T(1,128)} %bitcast.6, bf16[64,8192]{1,0:T(8,128)(2,1)} %bitcast.4, ...), custom_call_target="tpu_custom_call" | custom-call | tf_op jit(solution)/shard_map/pallas_call | solution.py:732
  71.6 1.0 %copy.12 = bf16[512,1024]{1,0:T(8,128)(2,1)} copy(bf16[512,1024]{1,0:T(8,128)(2,1)S(1)} %get-tuple-element.8) | data formatting | bytes 2097152

commit v3 on v2

--- a/solution.py
+++ b/solution.py
@@ -28,7 +28,7 @@
     1.0,
 )
 MESH = pl.DeviceIdType.MESH
-FAR, OWN, EARLY, YLAG, XLAG = 0, 14, 4, 4, 3
+OWN, EARLY, YLAG, XLAG = 14, 4, 4, 3
 
 
 def nibble_levels(words, plane):
@@ -44,7 +44,6 @@
 
 def plan(layers, pieces, groups, blocks):
     by_z = max(pieces // 2, pieces * 13 // 16)
-    far = max(pieces // 2, by_z - pieces // 16 * FAR)
     by_y = pieces // 2
     own_y = pieces * OWN // 16
     early = min(EARLY, own_y)
@@ -53,7 +52,7 @@
     group = pieces // groups
     spare = by_z - by_y
     turn = (layers - 3) * by_z + by_y
-    slots = turn + by_z + far - by_y
+    slots = turn + by_z + by_z - by_y
     ready = max(by_z, by_y + lag)
     per = -(-2 * groups // by_z)
     each = -(-blocks // (ready - 1))
@@ -78,7 +77,7 @@
         return turn + i if v == layers - 1 else (v - 1) * by_z + i
 
     last_x = turn + by_y + y_lag
-    total = max(slots, last_x + x_lag + pieces - far, own_slot(own_y - 1) + y_lag + 1)
+    total = max(slots, last_x + x_lag + pieces - by_z, own_slot(own_y - 1) + y_lag + 1)
     total = max(total, (layers - 4) * by_z + ready + -(-2 * groups // per))
 
     def seen(kind, i):
@@ -92,9 +91,8 @@
             when = 0
             for shorter in range((layers + 1) // 2):
                 hop = (v + 1) // 2 if v <= 2 * shorter else v - shorter
-                count = far if hop == layers - 1 else by_z
                 over = last_x + x_lag + twin if v == layers - 1 else send_slot(v, twin) + lag
-                when = max(when, z_slot(hop, i) if i < count else over)
+                when = max(when, z_slot(hop, i) if i < by_z else over)
             return when
         return send_slot(v, i) + y_lag if i < by_y else send_slot(v, twin) + lag
 
@@ -117,7 +115,6 @@
             tail.append((kind, g))
     return dict(
         by_z=by_z,
-        far=far,
         by_y=by_y,
         own_y=own_y,
         early=early,
@@ -168,7 +165,6 @@
     scale_ref,
     wide_gain_ref,
     low_ref,
-    share_ref,
     losses_ref,
     local_sem,
     z_send,
@@ -192,7 +188,7 @@
     p = plan(layers, pieces, groups, blocks)
     by_z, by_y, own_y, early = p["by_z"], p["by_y"], p["own_y"], p["early"]
     y_lag, lag, group, spare = p["y_lag"], p["lag"], p["group"], p["spare"]
-    slots, ready, far, turn = p["slots"], p["ready"], p["far"], p["turn"]
+    slots, ready, turn = p["slots"], p["ready"], p["turn"]
 
     sibling = (cx * 2 + 1 - cc, f)
     x_peer = ((1 - cx) * 2 + cc, f)
@@ -200,9 +196,6 @@
 
     def z_peer(step):
         return (g, (cl + step) * 2 + cy)
-
-    def by_hop(h):
-        return jnp.where(h == layers - 1, far, by_z)
 
     def inside(layer):
         return (layer >= 0) & (layer < layers)
@@ -246,36 +239,45 @@
         start = (layer * 2 + y) * rows + (q * 2 + c) * high
         return weight_ref.at[pl.ds(pl.multiple_of(start, high), high)]
 
+    def mine_slot(at, layer, q):
+        return jnp.where(layer > at, layer - 1, layer) * pieces + q
+
+    def other_slot(layer, q):
+        return (layers - 1 + layer) * pieces + q
+
     def slot(layer, y, q):
-        return (layer * 2 + y) * pieces + q
-
-    def link_copy(layer, y, q, send_sem, peer):
+        return jnp.where(y == cy, mine_slot(cl, layer, q), other_slot(layer, q))
+
+    def link_copy(layer, y, q, place, send_sem, peer):
         ref = chunk(layer, y, cc, q)
         return pltpu.make_async_remote_copy(
             src_ref=ref,
             dst_ref=ref,
             send_sem=send_sem,
-            recv_sem=link_recv.at[slot(layer, y, q)],
+            recv_sem=link_recv.at[place],
             device_id=peer,
             device_id_type=MESH,
         )
 
     def z_copy(layer, j, step):
-        sem = z_send.at[(1 + step) // 2 * layers + layer]
-        return link_copy(layer, cy, mirror(cx, j), sem, z_peer(step))
+        sem = z_send.at[jnp.where((layer == cl) & (step > 0), layers, layer)]
+        q = mirror(cx, j)
+        return link_copy(layer, cy, q, mine_slot(cl + step, layer, q), sem, z_peer(step))
 
     def x_piece(layer, y, j):
-        return link_copy(layer, y, mirror(cx, j), x_send.at[layer], x_peer)
+        q = mirror(cx, j)
+        return link_copy(layer, y, q, slot(layer, y, q), x_send.at[0], x_peer)
 
     def y_piece(layer, j):
-        return link_copy(layer, cy, mirror(cx, j), y_send.at[layer], y_peer)
+        q = mirror(cx, j)
+        return link_copy(layer, cy, q, other_slot(layer, q), y_send.at[0], y_peer)
 
     def core_copy(layer, y, q):
         ref = chunk(layer, y, cc, q)
         return pltpu.make_async_remote_copy(
             src_ref=ref,
             dst_ref=ref,
-            send_sem=core_send.at[layer * 2 + y],
+            send_sem=core_send.at[y],
             recv_sem=core_recv.at[(layer * 2 + y) * groups + q // group],
             device_id=sibling,
             device_id_type=MESH,
@@ -368,7 +370,7 @@
             j = index * group + i
             for step in (-1, 1):
 
-                @pl.when(inside(cl + step) & (j < by_hop(1)))
+                @pl.when(inside(cl + step) & (j < by_z))
                 def _():
                     z_copy(cl, j, step).start()
 
@@ -434,17 +436,19 @@
             low_ref[...].astype(jnp.bfloat16), up_ref[...], preferred_element_type=jnp.float32
         )
 
+    def whole(layer, y, index, is_own):
+        @pl.when(jnp.logical_not(is_own))
+        def _():
+            landed(some_rows(group), core_recv.at[(layer * 2 + y) * groups + index])
+
+    def product(layer, y, index):
+        size = rows // groups
+        at = pl.ds(pl.multiple_of((layer * 2 + y) * rows + index * size, size), size)
+        return jnp.dot(x_ref[:, at], weight_ref[at, :], preferred_element_type=jnp.float32)
+
     def multiply(layer, y, index, is_own):
-        size = rows // groups
-
-        @pl.when(jnp.logical_not(is_own))
-        def _():
-            landed(some_rows(group), core_recv.at[(layer * 2 + y) * groups + index])
-
-        at = pl.ds(pl.multiple_of((layer * 2 + y) * rows + index * size, size), size)
-        acc_ref[...] += jnp.dot(
-            x_ref[:, at], weight_ref[at, :], preferred_element_type=jnp.float32
-        )
+        whole(layer, y, index, is_own)
+        acc_ref[...] += product(layer, y, index)
 
     shorter = jnp.minimum(cl, layers - 1 - cl)
     longer = jnp.where(cl * 2 < layers - 1, 1, -1)
@@ -487,16 +491,16 @@
         for step in (-1, 1):
             layer = cl + step * s
 
-            @pl.when(inside(layer) & (j < by_hop(s)))
+            @pl.when(inside(layer))
             def _():
                 arrived(layer, cy, q)
-                go = inside(cl - step) & (j < by_hop(s + 1)) & jnp.logical_not(held(s, j))
+                go = inside(cl - step) & jnp.logical_not(held(s, j))
                 pl.when(go)(lambda: z_copy(layer, j, -step).start())
                 core_copy(layer, cy, q).start()
 
             if layers > 3:
                 layer_held = cl + step * (layers - 3)
-                waiting = (late >= by_y) & (late < by_z) & (late < by_hop(layers - 2))
+                waiting = (late >= by_y) & (late < by_z)
 
                 @pl.when(waiting & inside(layer_held) & inside(cl - step))
                 def _():
@@ -509,7 +513,7 @@
     def send_event(k):
         v, j = send_stage(k)
         layer = layer_of(v)
-        pl.when((v < layers - 1) & (j < pieces - by_hop(hops_of(v))))(
+        pl.when((v < layers - 1) & (j < pieces - by_z))(
             lambda: x_piece(layer, cy, j).start()
         )
         pl.when(j < by_y)(lambda: y_piece(layer, j).start())
@@ -540,7 +544,7 @@
         i = jnp.where(k < 0, o, j)
         q = mirror(1 - cx, i)
 
-        @pl.when((k >= 0) & (v < layers - 1) & (j < pieces - by_hop(hops_of(v))))
+        @pl.when((k >= 0) & (v < layers - 1) & (j < pieces - by_z))
         def _():
             arrived(layer, cy, q)
             core_copy(layer, cy, q).start()
@@ -553,7 +557,7 @@
     def last_x_event(k):
         v = layers - 1
         layer = layer_of(v)
-        count = pieces - by_hop(hops_of(v))
+        count = pieces - by_z
         j = k - p["last_x"]
         pl.when((j >= 0) & (j < count))(lambda: x_piece(layer, cy, j).start())
         i = j - p["x_lag"]
@@ -633,32 +637,28 @@
         return carry
 
     lax.fori_loop(0, p["total"], one_slot, 0)
-    for kind, index in p["tail"]:
+    target_copy.wait()
+    for kind, index in p["tail"][:-1]:
         layer, y = extra_of(jnp.int32(kind))
         multiply(layer, y, turned(index), kind == 0)
-
-    target_copy.wait()
-    share_ref[...] = jnp.zeros((8, 128), jnp.float32)
-
-    def finish(i, carry):
-        at = pl.ds(pl.multiple_of(i * block, block), block)
-        exact = acc_ref[at, :]
-        out_ref[at, :] = exact.astype(jnp.bfloat16)
-        error = exact - target_ref[at, :].astype(jnp.float32)
-        error = error * error
-        total = jnp.zeros((block, 128), jnp.float32)
-        for k in range(columns // 128):
-            total += error[:, k * 128 : (k + 1) * 128]
-        for k in range(block // 8):
-            share_ref[...] += total[k * 8 : (k + 1) * 8]
-        return carry
-
-    lax.fori_loop(0, tokens // block, finish, 0)
+    kind, index = p["tail"][-1]
+    layer, y = extra_of(jnp.int32(kind))
+    whole(layer, y, turned(index), kind == 0)
+    exact = acc_ref[...] + product(layer, y, turned(index))
+    out_ref[...] = exact.astype(jnp.bfloat16)
+    error = exact - target_ref[...].astype(jnp.float32)
+    error = error * error
+    total = jnp.zeros((tokens, 128), jnp.float32)
+    for k in range(columns // 128):
+        total += error[:, k * 128 : (k + 1) * 128]
+    share = jnp.zeros((8, 128), jnp.float32)
+    for k in range(tokens // 8):
+        share += total[k * 8 : (k + 1) * 8]
 
     fsdp = layers * 2
     members = 4 * fsdp
     spot = g * fsdp + f
-    losses_ref[spot] = jnp.sum(share_ref[...], axis=0, keepdims=True)
+    losses_ref[spot] = jnp.sum(share, axis=0, keepdims=True)
 
     def tell(j, carry):
         to = f + j
@@ -681,34 +681,21 @@
     lax.fori_loop(0, fsdp, tell, 0)
 
     def sent(layer, carry):
-        hops = jnp.abs(cl - layer)
-        for step in (-1, 1):
-
-            for count, test in ((far, hops == layers - 2), (by_z, hops < layers - 2)):
-
-                @pl.when(inside(cl + step) & ((cl - layer) * step >= 0) & test)
-                def _():
-                    landed(some_rows(count), z_send.at[(1 + step) // 2 * layers + layer])
-
-        @pl.when(layer == cl)
-        def _():
-            landed(some_rows(own_y), y_send.at[layer])
-            if own_y < pieces:
-                landed(some_rows(pieces - own_y), x_send.at[layer])
-
-        @pl.when(layer != cl)
-        def _():
-            landed(some_rows(by_y), y_send.at[layer])
-            for count, test in ((far, hops == layers - 1), (by_z, hops < layers - 1)):
-                pl.when(test)(
-                    lambda: landed(some_rows(pieces - count + by_y), x_send.at[layer])
-                )
-            landed(some_rows(pieces), core_send.at[layer * 2 + cy])
-
-        landed(some_rows(pieces), core_send.at[layer * 2 + 1 - cy])
+        up = inside(cl + 1) & (layer <= cl)
+        down = inside(cl - 1) & (layer >= cl)
+        own_up = up & (layer == cl)
+        pl.when(own_up)(lambda: landed(some_rows(by_z), z_send.at[layers]))
+        pl.when(down | (up & (layer != cl)))(
+            lambda: landed(some_rows(by_z), z_send.at[layer])
+        )
         return carry
 
     lax.fori_loop(0, layers, sent, 0)
+    away = layers - 1
+    landed(some_rows(away * by_y + own_y), y_send.at[0])
+    landed(some_rows(away * (by_y + pieces - by_z) + pieces - own_y), x_send.at[0])
+    landed(some_rows(away * pieces), core_send.at[cy])
+    landed(some_rows(layers * pieces), core_send.at[1 - cy])
     others = losses_ref.at[pl.ds(0, members - 1)]
     landed(others, loss_sem.at[1])
     everyone = jnp.sum(losses_ref[...], axis=0)
@@ -732,8 +719,8 @@
     kv, loss = pl.pallas_call(
         functools.partial(kernel, layers, pieces, groups),
         out_shape=(
-            jax.ShapeDtypeStruct((tokens, columns), jnp.bfloat16),
-            jax.ShapeDtypeStruct((1, 1), jnp.float32),
+            pltpu.VMEM((tokens, columns), jnp.bfloat16),
+            pltpu.VMEM((1, 1), jnp.float32),
         ),
         in_specs=[hbm] * 8,
         out_specs=(
@@ -756,14 +743,13 @@
             pltpu.VMEM(codes.shape, jnp.float32),
             pltpu.VMEM((width // 128, 128), jnp.float32),
             pltpu.VMEM((tokens, down.shape[1]), jnp.float32),
-            pltpu.VMEM((8, 128), jnp.float32),
             pltpu.VMEM((4 * fsdp, 1, 128), jnp.float32),
             dma((11,)),
-            dma((2 * layers,)),
-            dma((layers,)),
-            dma((layers,)),
-            dma((2 * layers,)),
-            dma((layers * 2 * pieces,)),
+            dma((layers + 1,)),
+            dma((1,)),
+            dma((1,)),
+            dma((2,)),
+            dma(((layers * 2 - 1) * pieces,)),
             dma((layers * 2 * groups,)),
             dma((2,)),
         ],

time: 74.6 us -> 72.9 us (0.977)
  Pallas kernels: 71 us -> 69.9 us
    pallas_call x1, Pallas kernels: 71 us -> 69.9 us  [per_device(): pl.pallas_call(functools.partial(kernel, layers, pieces, groups), out_sha...]
where the time goes in v3:
time: 72.9 us; the launch traced here: 72.6 us
  Pallas kernels  69.9 us (96%)
  between operations  1.8 us (2%)
  local copies, waits for them, and re-layouts  0.97 us (1%)
    pallas_call x1, Pallas kernels, per_device(): pl.pallas_call(functools.partial(kernel, layers, pieces, groups), out_sha...  69.9 us

profile of v3, /device:TPU:0, one launch (start us, length us, event | category | flops | bytes accessed | tf_op | source)
XLA Modules:
  0.0 72.6 jit_solution(7163473418361491999)
XLA Ops:
  0.6 69.9 %shard_map.95 = (bf16[512,1024]{1,0:T(8,128)(2,1)S(1)}, f32[1,1]{1,0:T(1,128)S(1)}) custom-call(bf16[512,8192]{1,0:T(8,128)(2,1)} %x_hbm.1, bf16[64,128]{1,0:T(8,128)(2,1)} %bitcast.5, s32[1024,256]{1,0:T(8,128)} %codes_hbm.1, s32[32,128]{1,0:T(8,128)} %scales_hbm.1, s32[1,64]{1,0:T(1,128)} %bitcast.6, bf16[64,8192]{1,0:T(8,128)(2,1)} %bitcast.4, ...), custom_call_target="tpu_custom_call" | custom-call | tf_op jit(solution)/shard_map/pallas_call | solution.py:719
  70.5 1.0 %copy.12 = bf16[512,1024]{1,0:T(8,128)(2,1)} copy(bf16[512,1024]{1,0:T(8,128)(2,1)S(1)} %get-tuple-element.6) | data formatting | bytes 2097152

commit v4 on v3

--- a/solution.py
+++ b/solution.py
@@ -100,7 +100,8 @@
     for kind in range(6):
         for g in range(groups):
             when = max(seen(kind, i) for i in range(g * group, (g + 1) * group))
-            items.append((max(when + 2, normal), kind, g))
+            when += 1 if when >= slots - 4 else 2
+            items.append((max(when, normal), kind, g))
     items.sort()
     extras, tail = [], []
     taken = {}

time: 72.9 us -> 72.5 us (level)
  no operation moved by 1% of the time
where the time goes in v4:
time: 72.5 us; the launch traced here: 72.3 us
  Pallas kernels  69.5 us (96%)
  between operations  1.8 us (2%)
  local copies, waits for them, and re-layouts  0.97 us (1%)
    pallas_call x1, Pallas kernels, per_device(): pl.pallas_call(functools.partial(kernel, layers, pieces, groups), out_sha...  69.5 us

profile of v4, /device:TPU:0, one launch (start us, length us, event | category | flops | bytes accessed | tf_op | source)
XLA Modules:
  0.0 72.3 jit_solution(11816006210905497913)
XLA Ops:
  0.6 69.5 %shard_map.95 = (bf16[512,1024]{1,0:T(8,128)(2,1)S(1)}, f32[1,1]{1,0:T(1,128)S(1)}) custom-call(bf16[512,8192]{1,0:T(8,128)(2,1)} %x_hbm.1, bf16[64,128]{1,0:T(8,128)(2,1)} %bitcast.5, s32[1024,256]{1,0:T(8,128)} %codes_hbm.1, s32[32,128]{1,0:T(8,128)} %scales_hbm.1, s32[1,64]{1,0:T(1,128)} %bitcast.6, bf16[64,8192]{1,0:T(8,128)(2,1)} %bitcast.4, ...), custom_call_target="tpu_custom_call" | custom-call | tf_op jit(solution)/shard_map/pallas_call | solution.py:720
  70.2 1.0 %copy.12 = bf16[512,1024]{1,0:T(8,128)(2,1)} copy(bf16[512,1024]{1,0:T(8,128)(2,1)S(1)} %get-tuple-element.6) | data formatting | bytes 2097152

commit v5 on v4

--- a/solution.py
+++ b/solution.py
@@ -213,7 +213,13 @@
     part = tokens // 4
     scales_copy = pltpu.make_async_copy(scales_hbm, scales_ref, local_sem.at[6])
     outer_copy = pltpu.make_async_copy(outer_hbm, outer_ref, local_sem.at[7])
-    codes_copy = pltpu.make_async_copy(codes_hbm, codes_ref, local_sem.at[8])
+
+    def codes_copy(index, place):
+        bunch = rows // groups
+        start = (index + cx * (groups - 1 - 2 * index)) * bunch
+        at = pl.ds(pl.multiple_of(start, bunch), bunch)
+        return pltpu.make_async_copy(codes_hbm.at[at], codes_ref.at[at], local_sem.at[place])
+
     gain_copy = pltpu.make_async_copy(gain_hbm, gain_ref, local_sem.at[9])
     up_copy = pltpu.make_async_copy(up_hbm, up_ref, local_sem.at[10])
     target_copy = pltpu.make_async_copy(target_hbm, target_ref, local_sem.at[4])
@@ -225,7 +231,9 @@
 
     scales_copy.start()
     outer_copy.start()
-    codes_copy.start()
+    codes_copy(0, 8).start()
+    for i in range(1, groups):
+        codes_copy(i, 10 + i).start()
     gain_copy.start()
     for i in range(4):
         x_copy(i).start()
@@ -380,7 +388,7 @@
     scales_copy.wait()
     outer_copy.wait()
     unpack(turned(0))
-    codes_copy.wait()
+    codes_copy(0, 8).wait()
     decode(cc, turned(0))
     neighbours = 3 + jnp.where(cl > 0, 1, 0) + jnp.where(cl < layers - 1, 1, 0)
     pl.semaphore_wait(barrier, neighbours)
@@ -388,6 +396,7 @@
 
     def rest(index, carry):
         unpack(turned(index))
+        codes_copy(index, 10 + index).wait()
         decode(cc, turned(index))
         own_sends(index)
         return carry
@@ -745,7 +754,7 @@
             pltpu.VMEM((width // 128, 128), jnp.float32),
             pltpu.VMEM((tokens, down.shape[1]), jnp.float32),
             pltpu.VMEM((4 * fsdp, 1, 128), jnp.float32),
-            dma((11,)),
+            dma((10 + groups,)),
             dma((layers + 1,)),
             dma((1,)),
             dma((1,)),

time: 72.5 us -> 72.3 us (level)
  no operation moved by 1% of the time
where the time goes in v5:
time: 72.3 us; the launch traced here: 72.1 us
  Pallas kernels  69.3 us (96%)
  between operations  1.8 us (2%)
  local copies, waits for them, and re-layouts  0.97 us (1%)
    pallas_call x1, Pallas kernels, per_device(): pl.pallas_call(functools.partial(kernel, layers, pieces, groups), out_sha...  69.3 us

profile of v5, /device:TPU:0, one launch (start us, length us, event | category | flops | bytes accessed | tf_op | source)
XLA Modules:
  0.0 72.1 jit_solution(3755970837041745752)
XLA Ops:
  0.6 69.3 %shard_map.95 = (bf16[512,1024]{1,0:T(8,128)(2,1)S(1)}, f32[1,1]{1,0:T(1,128)S(1)}) custom-call(bf16[512,8192]{1,0:T(8,128)(2,1)} %x_hbm.1, bf16[64,128]{1,0:T(8,128)(2,1)} %bitcast.5, s32[1024,256]{1,0:T(8,128)} %codes_hbm.1, s32[32,128]{1,0:T(8,128)} %scales_hbm.1, s32[1,64]{1,0:T(1,128)} %bitcast.6, bf16[64,8192]{1,0:T(8,128)(2,1)} %bitcast.4, ...), custom_call_target="tpu_custom_call" | custom-call | tf_op jit(solution)/shard_map/pallas_call | solution.py:729
  70.0 1.0 %copy.12 = bf16[512,1024]{1,0:T(8,128)(2,1)} copy(bf16[512,1024]{1,0:T(8,128)(2,1)S(1)} %get-tuple-element.6) | data formatting | bytes 2097152
